TPU v7x, 32 devices: a whole 2x2x4 slice. The times are simulated.
32 devices in a mesh: kgrp: 8 (over y, x, core), img: 4 (over z).
Axes of the slice: x: 2, y: 2, z: 4, core: 2. Of those that a mesh axis runs over, the one named last changes fastest.
Arguments:
- vectors: float32 [2, 16, 1024], P(None, 'img', 'kgrp'), may hold values from -6 to 6
- conduction: bfloat16 [16, 2, 8, 4, 4096], P('kgrp', None, None, 'img'), may hold values from -6 to 6
- valence: bfloat16 [16, 2, 8, 4, 4096], P('kgrp', None, None, 'img'), may hold values from -6 to 6
- hole_point: int32 [1], replicated, may hold values from 0 to 16383
- kpoint_grid: int32 [3, 16], replicated, may hold values from 0 to 11
- image_cells: int32 [3, 512], replicated, may hold values from -6 to 6
Outputs:
- psi_real: float32 [16, 4, 4096, 512], P(None, 'img', 'kgrp')
- psi_imag: float32 [16, 4, 4096, 512], P(None, 'img', 'kgrp')
All inputs are finite; a program needn't handle non-finite values.
Results may differ from a plain program's by a relative error of at most 0.0043.
Values may be sent and summed in bfloat16 or wider, within the bound.
No kernel may reach another device: no remote copies, remote signals or barrier semaphores. Data moves between devices by JAX's collectives and lax.ppermute only.
A program may use at most 128 MiB of HBM per device.

v0:
```python
import jax
import jax.numpy as jnp
import numpy as np
from jax import lax
from jax.sharding import PartitionSpec as P

NV = 8
NC = 8
cosine_levels = np.cos(2.0 * np.pi * np.arange(12) / 12.0)
sine_levels = np.sin(2.0 * np.pi * np.arange(12) / 12.0)


def phase_table(kpoint_grid, image_cells):
    turn_count = kpoint_grid[0][:, None] * image_cells[0][None, :]
    turn_count = turn_count + kpoint_grid[1][:, None] * image_cells[1][None, :]
    turn_count = turn_count + kpoint_grid[2][:, None] * image_cells[2][None, :]
    turn_count = jnp.mod(turn_count, 12)
    cosine = jnp.zeros(turn_count.shape, jnp.float32)
    sine_part = jnp.zeros(turn_count.shape, jnp.float32)
    for level_index in range(12):
        matches = turn_count == level_index
        cosine = jnp.where(matches, jnp.float32(cosine_levels[level_index]), cosine)
        sine_part = jnp.where(matches, jnp.float32(sine_levels[level_index]), sine_part)
    upper_half = jnp.stack([cosine, sine_part], 1)
    lower_half = jnp.stack([-sine_part, cosine], 1)
    return jnp.stack([upper_half, lower_half], 0).astype(jnp.bfloat16)


def hole_weights(amplitudes, hole_values):
    norm_factor = (NV * NC) ** (-0.5)
    real_amplitude = amplitudes[0]
    imaginary_amplitude = amplitudes[1]
    real_hole = hole_values[:, 0]
    imaginary_hole = hole_values[:, 1]
    highest = lax.Precision.HIGHEST
    weight_real = jnp.einsum("skvc,kv->ksc", real_amplitude, real_hole, precision=highest)
    weight_real = weight_real + jnp.einsum(
        "skvc,kv->ksc", imaginary_amplitude, imaginary_hole, precision=highest
    )
    weight_imaginary = jnp.einsum("skvc,kv->ksc", imaginary_amplitude, real_hole, precision=highest)
    weight_imaginary = weight_imaginary - jnp.einsum(
        "skvc,kv->ksc", real_amplitude, imaginary_hole, precision=highest
    )
    return jnp.stack([weight_real * norm_factor, weight_imaginary * norm_factor], 1).astype(
        jnp.bfloat16
    )


def mixing(weights):
    weight_real = weights[:, 0]
    weight_imaginary = weights[:, 1]
    first_row = jnp.stack([weight_real, -weight_imaginary], 2)
    second_row = jnp.stack([weight_imaginary, weight_real], 2)
    return jnp.stack([first_row, second_row], 1)


def shards(vectors, conduction, valence, hole_point, kpoint_grid, image_cells):
    group_size = lax.axis_size("kgrp")
    local_k = conduction.shape[0]
    slab_width = conduction.shape[4]
    own_excitons = vectors.shape[1]
    blocks = vectors.shape[2] // group_size
    columns = vectors.reshape(2, own_excitons, group_size, blocks)
    owned_columns = lax.all_to_all(columns, "kgrp", split_axis=2, concat_axis=2, tiled=True)
    owned_columns = owned_columns.reshape(2, own_excitons, local_k, NV, NC)
    hole_offset = hole_point[0] % slab_width
    hole_slab = hole_point[0] // slab_width
    present = (lax.axis_index("img") == hole_slab).astype(jnp.float32)
    picked = (
        lax.dynamic_slice_in_dim(valence[:, :, :, 0, :], hole_offset, 1, 3)[..., 0].astype(
            jnp.float32
        )
        * present
    )
    hole_values = lax.psum(picked, "img")
    weights = lax.all_gather(hole_weights(owned_columns, hole_values), "img", axis=2, tiled=True)
    phases = phase_table(kpoint_grid, image_cells)
    products = jnp.einsum(
        "kasbc,kbcp->sakp",
        mixing(weights),
        conduction[:, :, :, 0, :],
        preferred_element_type=jnp.float32,
    ).astype(jnp.bfloat16)
    summed = jnp.einsum(
        "sakp,akbn->spbn",
        lax.all_to_all(products, "kgrp", split_axis=3, concat_axis=2, tiled=True),
        phases,
        preferred_element_type=jnp.float32,
    )
    normal_scale = (2 * kpoint_grid.shape[1]) ** (-0.5)
    summed = summed * normal_scale
    return (summed[:, None, :, 0, :], summed[:, None, :, 1, :])


def solution(mesh):
    placed = (
        P(None, "img", "kgrp"),
        P("kgrp", None, None, "img", None),
        P("kgrp", None, None, "img", None),
        P(),
        P(),
        P(),
    )
    return jax.shard_map(
        shards,
        mesh=mesh,
        in_specs=placed,
        out_specs=(P(None, "img", "kgrp", None), P(None, "img", "kgrp", None)),
        check_vma=False,
    )
```

profile of v0, /device:TPU:0, one launch (start us, length us, event | category | flops | bytes accessed | tf_op | source)
XLA Modules:
  0.0 113.5 jit_solution(17862852057084318996)
XLA Ops:
  0.6 0.0 copy-start
  0.6 0.8 reshape.639
  1.5 0.7 reshape.653
  2.2 5.2 %all-to-all-start = ((f32[8,1,128]{2,1,0:T(1,128)}), f32[8,1,128]{2,1,0:T(1,128)S(1)}, u32[]{:S(2)}, u32[]{:S(2)}) async-start(f32[8,1,128]{2,1,0:T(1,128)} %reshape.653), calls=%async_computation | async-start | bytes 8192 | tf_op jit(solution)/shard_map/all_to_all | solution.py:64
  7.4 0.8 fusion.27
  8.9 0.9 multiply_reduce_fusion
  9.7 11.9 %psum.7 = f32[2,2,8]{2,1,0:T(2,128)S(1)} all-reduce(f32[2,2,8]{2,1,0:T(2,128)S(1)} %multiply_reduce_fusion), channel_id=1, replica_groups=mesh['kgrp'=8,'img'=4] {'img'}, use_global_device_ids=true, to_apply=%region_0.1 | all-reduce | flops 32 | bytes 256 | tf_op jit(solution)/shard_map/psum | solution.py:75
  21.7 0.0 all-to-all-done
  21.7 0.5 broadcast.739
  22.2 0.7 reduce.2
  22.8 0.1 reshape.654
  23.0 0.1 squeeze.26
  23.0 0.2 fusion.13
  23.2 0.2 fusion.15
  23.4 0.1 squeeze.28
  23.4 0.2 fusion.9
  23.6 0.2 fusion.11
  23.8 13.2 %all_gather.3 = bf16[2,2,16,8]{3,1,0,2:T(2,128)(2,1)S(1)} all-gather(bf16[2,2,4,8]{3,1,0,2:T(2,128)(2,1)S(1)} %copy.34), channel_id=1, replica_groups=mesh['kgrp'=8,'img'=4] {'img'}, dimensions={2}, use_global_device_ids=true | all-gather | bytes 1280 | tf_op jit(solution)/shard_map/all_gather | solution.py:76
  37.1 0.1 copy.56
  37.2 0.1 copy.55
  37.3 0.0 copy-done
  37.3 0.3 fusion.1
  37.6 6.9 %copy.38 = bf16[16,2,2,4096]{0,1,2,3:T(2,128)(2,1)} copy(bf16[16,2,2,4096]{3,0,1,2:T(8,128)(2,1)S(1)} %fusion.1) | data formatting | bytes 1048576 | tf_op jit(solution)/shard_map/convert_element_type | solution.py:83
  44.5 6.5 %reshape.655 = bf16[8,2,16384]{2,1,0:T(2,128)(2,1)} reshape(bf16[4096,2,2,16]{3,2,1,0:T(2,128)(2,1)} %bitcast.101) | data formatting | bytes 1048576
  51.0 4.2 %all-to-all-start.1 = ((bf16[8,2,16384]{2,1,0:T(2,128)(2,1)}), bf16[8,2,16384]{2,1,0:T(2,128)(2,1)S(1)}, u32[]{:S(2)}, u32[]{:S(2)}) async-start(bf16[8,2,16384]{2,1,0:T(2,128)(2,1)} %reshape.655), calls=%async_computation.1 | async-start | bytes 1048576 | tf_op jit(solution)/shard_map/all_to_all | solution.py:86
  55.2 0.8 slice_bitcast_fusion.6
  56.0 0.1 fusion.20
  56.1 8.8 %all-to-all-done.1 = bf16[8,2,16384]{2,1,0:T(2,128)(2,1)S(1)} async-done(((bf16[8,2,16384]{2,1,0:T(2,128)(2,1)}), bf16[8,2,16384]{2,1,0:T(2,128)(2,1)S(1)}, u32[]{:S(2)}, u32[]{:S(2)}) %all-to-all-start.1) | async-done | bytes 524320 | tf_op jit(solution)/shard_map/all_to_all | solution.py:86
  64.9 4.1 %reshape.656 = bf16[4096,2,2,16]{3,2,1,0:T(2,128)(2,1)} reshape(bf16[8,2,16384]{2,1,0:T(2,128)(2,1)S(1)} %all-to-all-done.1) | data formatting | bytes 1048576
  68.9 9.7 %copy.39 = bf16[16,2,2,8,512]{4,2,3,1,0:T(2,128)(2,1)S(1)} copy(bf16[16,2,2,8,512]{0,1,2,4,3:T(2,128)(2,1)} %bitcast.102) | data formatting | bytes 1048576 | tf_op jit(solution)/shard_map/all_to_all | solution.py:86
  78.7 0.2 reshape.648
  78.9 13.1 %bitcast_multiply_fusion = f32[16,512,2,512]{3,1,2,0:T(8,128)} fusion(bf16[16,2,16,512,1]{3,2,1,0,4:T(8,128)(2,1)S(1)} %reshape.648, bf16[1,16,2,512]{3,1,0,2:T(8,128)(2,1)S(1)} %get-tuple-element.15, bf16[1,16,2,512]{3,1,0,2:T(8,128)(2,1)S(1)} %get-tuple-element.14), kind=kOutput, calls=%fused_computation | convolution fusion | flops 545390592 | bytes 34144256 | tf_op jit(solution)/shard_map/sakp,akbn->spbn/dot_general | solution.py:84
  91.9 0.0 copy-start.1
  91.9 21.5 %slice_bitcast_fusion = (f32[16,1,512,512]{3,2,1,0:T(8,128)}, f32[16,1,512,512]{3,2,1,0:T(8,128)}) fusion(f32[16,512,2,512]{3,1,2,0:T(8,128)} %bitcast_multiply_fusion), kind=kLoop, calls=%fused_computation.1 | loop fusion | bytes 67108864
  113.5 0.0 copy-done.1
  (11 shorter events, 0.1 us)
Async XLA Ops:
  0.6 36.6 %copy-start = (bf16[2,2,8,1,4096]{4,2,3,1,0:T(8,128)(2,1)S(1)}, bf16[2,2,8,1,4096]{4,2,3,1,0:T(8,128)(2,1)}, u32[]{:S(2)}) copy-start(bf16[2,2,8,1,4096]{4,2,3,1,0:T(8,128)(2,1)} %param.7) | copy-start | bytes 786436
  2.2 19.5 %all-to-all-start = ((f32[8,1,128]{2,1,0:T(1,128)}), f32[8,1,128]{2,1,0:T(1,128)S(1)}, u32[]{:S(2)}, u32[]{:S(2)}) async-start(f32[8,1,128]{2,1,0:T(1,128)} %reshape.653), calls=%async_computation | async-start | bytes 8192 | tf_op jit(solution)/shard_map/all_to_all | solution.py:64
  51.0 13.9 %all-to-all-start.1 = ((bf16[8,2,16384]{2,1,0:T(2,128)(2,1)}), bf16[8,2,16384]{2,1,0:T(2,128)(2,1)S(1)}, u32[]{:S(2)}, u32[]{:S(2)}) async-start(bf16[8,2,16384]{2,1,0:T(2,128)(2,1)} %reshape.655), calls=%async_computation.1 | async-start | bytes 1048576 | tf_op jit(solution)/shard_map/all_to_all | solution.py:86
  91.9 21.5 %copy-start.1 = (bf16[2,2,8,1,4096]{4,2,3,1,0:T(8,128)(2,1)S(1)}, bf16[2,2,8,1,4096]{4,2,3,1,0:T(8,128)(2,1)}, u32[]{:S(2)}) copy-start(bf16[2,2,8,1,4096]{4,2,3,1,0:T(8,128)(2,1)} %param.7) | copy-start | bytes 786436
where the time goes:
time: 114 us; the launch traced here: 113 us
  local copies, waits for them, and re-layouts  53 us (46%)
  blocking collectives  25.2 us (22%)
  matrix products  14.1 us (12%)
  starting transfers between devices  9.4 us (8%)
  waiting for transfers between devices  8.76 us (8%)
  other arithmetic  1.71 us (2%)
  between operations  1.44 us (1%)
    unnamed x11, local copies, waits for them, and re-layouts  33 us
    all_gather x1, blocking collectives, shards(): lax.all_gather(hole_weights(owned_columns, hole_values), 'img', axis=2, t...  13.2 us
    dot_general x1, matrix products, shards(): jnp.einsum('sakp,akbn->spbn', lax.all_to_all(products, 'kgrp', split_axis...  13.1 us
    psum x1, blocking collectives, shards(): hole_values = lax.psum(picked, 'img')  11.9 us
    all_to_all x2, local copies, waits for them, and re-layouts, shards(): lax.all_to_all(products, 'kgrp', split_axis=3, concat_axis=2, tiled=True)  9.93 us
    all_to_all x1, waiting for transfers between devices, shards(): lax.all_to_all(products, 'kgrp', split_axis=3, concat_axis=2, tiled=True)  8.76 us
    convert_element_type x1, local copies, waits for them, and re-layouts, shards(): products = jnp.einsum('kasbc,kbcp->sakp', mixing(weights), conduction[:,...  6.9 us
    all_to_all x1, starting transfers between devices, shards(): lax.all_to_all(columns, 'kgrp', split_axis=2, concat_axis=2, tiled=True)  5.2 us
  transfers between devices with their start and end apart: 2, of which 1 were waited for; matrix products, arithmetic and copies ran while one was open for 2% of the time, Pallas kernels for 0%

commit v1 on v0

--- a/solution.py
+++ b/solution.py
@@ -8,6 +8,16 @@
 NC = 8
 cosine_levels = np.cos(2.0 * np.pi * np.arange(12) / 12.0)
 sine_levels = np.sin(2.0 * np.pi * np.arange(12) / 12.0)
+
+
+def steps_all_work(patch):
+    heard = jnp.concatenate(
+        lax.all_to_all(
+            jnp.stack(jnp.split(patch, lax.axis_size("kgrp"), axis=3), axis=0), "kgrp", 0, 0
+        ),
+        axis=2,
+    )
+    return heard
 
 
 def phase_table(kpoint_grid, image_cells):
@@ -82,10 +92,7 @@
         preferred_element_type=jnp.float32,
     ).astype(jnp.bfloat16)
     summed = jnp.einsum(
-        "sakp,akbn->spbn",
-        lax.all_to_all(products, "kgrp", split_axis=3, concat_axis=2, tiled=True),
-        phases,
-        preferred_element_type=jnp.float32,
+        "sakp,akbn->spbn", steps_all_work(products), phases, preferred_element_type=jnp.float32
     )
     normal_scale = (2 * kpoint_grid.shape[1]) ** (-0.5)
     summed = summed * normal_scale

time: 114 us -> 91.6 us (0.80)
  local copies, waits for them, and re-layouts: 53 us -> 30.7 us
    all_to_all x2 -> x0, local copies, waits for them, and re-layouts: 9.93 us -> none  [shards(): lax.all_to_all(products, 'kgrp', split_axis=3, concat_axis=2, tiled=True)]
    convert_element_type x1 -> x0, local copies, waits for them, and re-layouts: 6.9 us -> none  [shards(): products = jnp.einsum('kasbc,kbcp->sakp', mixing(weights), conduction[:,...]
    unnamed x11 -> x16, local copies, waits for them, and re-layouts: 33 us -> 26.9 us
  transfers between devices with their start and end apart: 2 -> 2, of which waited for: 1 -> 1; matrix products, arithmetic and copies ran while one was open for 2% -> 3% of each run, Pallas kernels for 0% -> 0%
where the time goes in v1:
time: 91.6 us; the launch traced here: 91.2 us
  local copies, waits for them, and re-layouts  30.7 us (34%)
  blocking collectives  25.2 us (28%)
  matrix products  14.1 us (15%)
  starting transfers between devices  9.4 us (10%)
  waiting for transfers between devices  8.76 us (10%)
  other arithmetic  1.71 us (2%)
  between operations  1.43 us (2%)
    unnamed x16, local copies, waits for them, and re-layouts  26.9 us
    all_gather x1, blocking collectives, shards(): lax.all_gather(hole_weights(owned_columns, hole_values), 'img', axis=2, t...  13.2 us
    dot_general x1, matrix products, shards(): jnp.einsum('sakp,akbn->spbn', steps_all_work(products), phases, preferred...  13.1 us
    psum x1, blocking collectives, shards(): hole_values = lax.psum(picked, 'img')  11.9 us
    all_to_all x1, waiting for transfers between devices, steps_all_work(): lax.all_to_all(jnp.stack(jnp.split(patch, lax.axis_size('kgrp'), axis=3),...  8.76 us
    all_to_all x1, starting transfers between devices, shards(): lax.all_to_all(columns, 'kgrp', split_axis=2, concat_axis=2, tiled=True)  5.2 us
    all_to_all x1, starting transfers between devices, steps_all_work(): lax.all_to_all(jnp.stack(jnp.split(patch, lax.axis_size('kgrp'), axis=3),...  4.2 us
  transfers between devices with their start and end apart: 2, of which 1 were waited for; matrix products, arithmetic and copies ran while one was open for 3% of the time, Pallas kernels for 0%

profile of v1, /device:TPU:0, one launch (start us, length us, event | category | flops | bytes accessed | tf_op | source)
XLA Modules:
  0.0 91.2 jit_solution(5312893566767054547)
XLA Ops:
  0.6 0.0 copy-start
  0.6 0.8 reshape.645
  1.5 0.7 reshape.660
  2.2 5.2 %all-to-all-start = ((f32[8,1,128]{2,1,0:T(1,128)}), f32[8,1,128]{2,1,0:T(1,128)S(1)}, u32[]{:S(2)}, u32[]{:S(2)}) async-start(f32[8,1,128]{2,1,0:T(1,128)} %reshape.660), calls=%async_computation | async-start | bytes 8192 | tf_op jit(solution)/shard_map/all_to_all | solution.py:74
  7.4 0.8 fusion.35
  8.9 0.9 multiply_reduce_fusion
  9.7 11.9 %psum.7 = f32[2,2,8]{2,1,0:T(2,128)S(1)} all-reduce(f32[2,2,8]{2,1,0:T(2,128)S(1)} %multiply_reduce_fusion), channel_id=1, replica_groups=mesh['kgrp'=8,'img'=4] {'img'}, use_global_device_ids=true, to_apply=%region_0.1 | all-reduce | flops 32 | bytes 256 | tf_op jit(solution)/shard_map/psum | solution.py:85
  21.7 0.0 all-to-all-done
  21.7 0.5 broadcast.739
  22.2 0.7 reduce.2
  22.8 0.1 reshape.661
  23.0 0.1 squeeze.26
  23.0 0.2 fusion.21
  23.2 0.2 fusion.23
  23.4 0.1 squeeze.28
  23.4 0.2 fusion.17
  23.6 0.2 fusion.19
  23.8 13.2 %all_gather.3 = bf16[2,2,16,8]{3,1,0,2:T(2,128)(2,1)S(1)} all-gather(bf16[2,2,4,8]{3,1,0,2:T(2,128)(2,1)S(1)} %copy.33), channel_id=1, replica_groups=mesh['kgrp'=8,'img'=4] {'img'}, dimensions={2}, use_global_device_ids=true | all-gather | bytes 1280 | tf_op jit(solution)/shard_map/all_gather | solution.py:86
  37.1 0.1 copy.56
  37.2 0.1 copy.55
  37.3 0.0 copy-done
  37.3 0.3 fusion.1
  37.6 0.6 fusion.11
  38.2 0.6 fusion.10
  38.9 0.6 fusion.9
  39.5 0.6 fusion.8
  40.1 0.6 fusion.7
  40.8 0.6 fusion.6
  41.4 0.6 fusion.5
  42.0 0.6 fusion.4
  42.7 4.2 %all-to-all-start.1 = ((bf16[8,16,2,2,512]{4,1,2,3,0:T(8,128)(2,1)}), bf16[8,16,2,2,512]{4,1,2,3,0:T(8,128)(2,1)S(1)}, u32[]{:S(2)}, u32[]{:S(2)}) async-start(bf16[8,16,2,2,512]{4,1,2,3,0:T(8,128)(2,1)} %fusion.4), calls=%async_computation.1 | async-start | bytes 1048576 | tf_op jit(solution)/shard_map/all_to_all | solution.py:15
  46.9 0.8 slice_bitcast_fusion.14
  47.7 0.1 fusion.28
  47.8 8.8 %all-to-all-done.1 = bf16[8,16,2,2,512]{4,1,2,3,0:T(8,128)(2,1)S(1)} async-done(((bf16[8,16,2,2,512]{4,1,2,3,0:T(8,128)(2,1)}), bf16[8,16,2,2,512]{4,1,2,3,0:T(8,128)(2,1)S(1)}, u32[]{:S(2)}, u32[]{:S(2)}) %all-to-all-start.1) | async-done | bytes 524320 | tf_op jit(solution)/shard_map/all_to_all | solution.py:15
  56.6 0.0 copy-start.1
  56.6 13.1 %bitcast_multiply_fusion = f32[16,512,2,512]{3,1,2,0:T(8,128)} fusion(bf16[16,2,16,512,1]{3,0,1,2,4:T(8,128)(2,1)S(1)} %bitcast.131, bf16[1,16,2,512]{3,1,0,2:T(8,128)(2,1)S(1)} %get-tuple-element.15, bf16[1,16,2,512]{3,1,0,2:T(8,128)(2,1)S(1)} %get-tuple-element.14), kind=kOutput, calls=%fused_computation | convolution fusion | flops 545390592 | bytes 34144256 | tf_op jit(solution)/shard_map/sakp,akbn->spbn/dot_general | solution.py:94
  69.7 21.5 %slice_bitcast_fusion = (f32[16,1,512,512]{3,2,1,0:T(8,128)}, f32[16,1,512,512]{3,2,1,0:T(8,128)}) fusion(f32[16,512,2,512]{3,1,2,0:T(8,128)} %bitcast_multiply_fusion), kind=kLoop, calls=%fused_computation.1 | loop fusion | bytes 67108864
  91.2 0.0 copy-done.1
  (11 shorter events, 0.1 us)
Async XLA Ops:
  0.6 36.6 %copy-start = (bf16[2,2,8,1,4096]{4,2,3,1,0:T(8,128)(2,1)S(1)}, bf16[2,2,8,1,4096]{4,2,3,1,0:T(8,128)(2,1)}, u32[]{:S(2)}) copy-start(bf16[2,2,8,1,4096]{4,2,3,1,0:T(8,128)(2,1)} %param.7) | copy-start | bytes 786436
  2.2 19.5 %all-to-all-start = ((f32[8,1,128]{2,1,0:T(1,128)}), f32[8,1,128]{2,1,0:T(1,128)S(1)}, u32[]{:S(2)}, u32[]{:S(2)}) async-start(f32[8,1,128]{2,1,0:T(1,128)} %reshape.660), calls=%async_computation | async-start | bytes 8192 | tf_op jit(solution)/shard_map/all_to_all | solution.py:74
  42.7 13.9 %all-to-all-start.1 = ((bf16[8,16,2,2,512]{4,1,2,3,0:T(8,128)(2,1)}), bf16[8,16,2,2,512]{4,1,2,3,0:T(8,128)(2,1)S(1)}, u32[]{:S(2)}, u32[]{:S(2)}) async-start(bf16[8,16,2,2,512]{4,1,2,3,0:T(8,128)(2,1)} %fusion.4), calls=%async_computation.1 | async-start | bytes 1048576 | tf_op jit(solution)/shard_map/all_to_all | solution.py:15
  56.6 34.6 %copy-start.1 = (bf16[2,2,8,1,4096]{4,2,3,1,0:T(8,128)(2,1)S(1)}, bf16[2,2,8,1,4096]{4,2,3,1,0:T(8,128)(2,1)}, u32[]{:S(2)}) copy-start(bf16[2,2,8,1,4096]{4,2,3,1,0:T(8,128)(2,1)} %param.7) | copy-start | bytes 786436
